TPU v7x, 32 devices: a whole 2x2x4 slice. The times are simulated.
32 devices in a mesh: section: 4 (over y, x), seq: 8 (over z, core).
Axes of the slice: x: 2, y: 2, z: 4, core: 2. Of those that a mesh axis runs over, the one named last changes fastest.
Arguments:
- stream: bfloat16 [4, 128, 1536], P('section', 'seq'), may hold values from -6 to 6
- queries: bfloat16 [4, 128, 1536], P('section', 'seq'), may hold values from -40 to 40
- fresh_keys: bfloat16 [4, 128, 1536], P('section', 'seq'), may hold values from -4 to 4
- fresh_values: bfloat16 [4, 128, 1536], P('section', 'seq'), may hold values from -6 to 6
- stale_keys: bfloat16 [4, 1536, 1536], P('section', 'seq'), may hold values from -6 to 6
- stale_values: bfloat16 [4, 1536, 1536], P('section', 'seq'), may hold values from -6 to 6
- gate: float32 [4, 1536], P('section'), may hold values from 0.5 to 4
- patch_of_section: int32 [4], P('section'), may hold values from 0 to 7, as said below
- text_len: int32 [1], replicated, may hold values from 128 to 512
Outputs:
- attended: bfloat16 [4, 128, 1536], P('section', 'seq')
- stream_next: bfloat16 [4, 128, 1536], P('section', 'seq')
Inputs may be any that keep to these rules, and one draw needn't show every extreme that they name: `patch_of_section`: section s works on patch (c - s) mod 8 for one c of the draw. The first text_len text positions are used.
All inputs are finite; a program needn't handle non-finite values.
Results may differ from a plain program's by a relative error of at most 0.0085.
Values may be sent and summed in bfloat16 or wider, within the bound.
A program may use at most 64 MiB of HBM per device.

v0:
```python
import math
import jax
import jax.numpy as jnp
from jax import lax
from jax.sharding import PartitionSpec as P

HEADS = 12
HDIM = 128
TXT = 512
FLOOR_SCORE = -1e30


def passed_along(value, axis, steps):
    count = lax.axis_size(axis)
    pairs = [(source, (source + steps) % count) for source in range(count)]
    return lax.ppermute(value, axis, pairs)


def head_scores(query_rows, key_rows):
    query_heads = query_rows.reshape(query_rows.shape[0], HEADS, HDIM)
    key_heads = key_rows.reshape(key_rows.shape[0], HEADS, HDIM)
    return jnp.einsum(
        "qhd,khd->hqk", query_heads, key_heads, preferred_element_type=jnp.float32
    ) / math.sqrt(HDIM)


def weighted_values(weights, value_rows):
    value_heads = value_rows.reshape(value_rows.shape[0], HEADS, HDIM)
    return jnp.einsum(
        "hqk,khd->qhd",
        weights.astype(jnp.bfloat16),
        value_heads,
        preferred_element_type=jnp.float32,
    )


def stale_allowed(first_row, piece_rows, patch_index, text_count, patch_length):
    positions = first_row + jnp.arange(piece_rows, dtype=jnp.int32)
    region = (positions - TXT) // patch_length
    return jnp.where(positions < TXT, positions < text_count, region != patch_index)


def local(
    stream,
    queries,
    fresh_keys,
    fresh_values,
    stale_keys,
    stale_values,
    gate,
    patch_of_section,
    text_len,
):
    incoming = passed_along(stream, "section", 1)
    row_count = queries.shape[1]
    patch_length = row_count * lax.axis_size("seq")
    patch_index = patch_of_section[0]
    text_count = text_len[0]
    everyone = lax.all_gather(queries, "seq", axis=1, tiled=True)[0]
    stale_rows = stale_keys.shape[1]
    key_rows = jnp.concatenate([stale_keys[0], fresh_keys[0]], 0)
    value_rows = jnp.concatenate([stale_values[0], fresh_values[0]], 0)
    first_row = lax.axis_index("seq") * stale_rows
    allowed = jnp.concatenate(
        [
            stale_allowed(first_row, stale_rows, patch_index, text_count, patch_length),
            jnp.ones((row_count,), dtype=bool),
        ],
        0,
    )
    scores = jnp.where(allowed[None, None, :], head_scores(everyone, key_rows), FLOOR_SCORE)
    local_max = jnp.max(scores, axis=2)
    global_max = lax.pmax(local_max, "seq")
    weights = jnp.where(allowed[None, None, :], jnp.exp(scores - local_max[:, :, None]), 0.0)
    factor = jnp.exp(local_max - global_max)
    partial_value = weighted_values(weights, value_rows) * jnp.transpose(factor)[:, :, None]
    partial_value = partial_value.reshape(patch_length, HEADS * HDIM)
    weight_sums = jnp.transpose(jnp.sum(weights, axis=2) * factor)
    weighted, row_sums = (
        lax.psum_scatter(partial_value, "seq", scatter_dimension=0, tiled=True),
        lax.psum_scatter(weight_sums, "seq", scatter_dimension=0, tiled=True),
    )
    averaged = weighted.reshape(row_count, HEADS, HDIM) / row_sums[:, :, None]
    attended = averaged.reshape(1, row_count, HEADS * HDIM).astype(jnp.bfloat16)
    stream_next = (
        incoming.astype(jnp.float32) + gate[:, None, :] * attended.astype(jnp.float32)
    ).astype(jnp.bfloat16)
    return (attended, stream_next)


def solution(mesh):
    placed = (
        P("section", "seq", None),
        P("section", "seq", None),
        P("section", "seq", None),
        P("section", "seq", None),
        P("section", "seq", None),
        P("section", "seq", None),
        P("section", None),
        P("section"),
        P(),
    )
    return jax.shard_map(
        local,
        mesh=mesh,
        in_specs=placed,
        out_specs=(P("section", "seq", None), P("section", "seq", None)),
        check_vma=False,
    )
```

profile of v0, /device:TPU:0, one launch (start us, length us, event | category | flops | bytes accessed | tf_op | source)
XLA Modules:
  0.0 116.1 jit_solution(6922269851643474781)
XLA Ops:
  7.2 0.0 reduce-scatter.7.cloned.1.call-start
  8.5 0.0 copy-start.1
  8.5 1.5 %concatenate.23 = bf16[192,12,128]{2,1,0:T(8,128)(2,1)S(1)} reshape(bf16[1,192,1536]{2,1,0:T(8,128)(2,1)} %param.13) | data formatting | bytes 1179648 | tf_op jit(solution)/shard_map/concatenate | solution.py:61
  10.0 0.0 copy-start.2
  10.0 0.2 copy.23
  10.2 0.0 copy-done.1
  10.2 16.2 %all_gather.3 = bf16[1,128,1536]{2,1,0:T(8,128)(2,1)S(1)} all-gather(bf16[1,16,1536]{2,1,0:T(8,128)(2,1)S(1)} %copy-done.1), channel_id=1, replica_groups=mesh['section'=4,'seq'=8] {'seq'}, dimensions={1}, use_global_device_ids=true | all-gather | bytes 442368 | tf_op jit(solution)/shard_map/all_gather | solution.py:59
  26.4 0.2 copy.25
  26.7 0.1 concatenate.24
  26.8 0.5 fusion.22
  27.3 0.0 copy-start
  27.3 17.3 %pmax.7 = f32[12,128]{1,0:T(8,128)S(1)} all-reduce(f32[12,128]{1,0:T(8,128)S(1)} %get-tuple-element.6), channel_id=1, replica_groups=mesh['section'=4,'seq'=8] {'seq'}, use_global_device_ids=true, to_apply=%region_1.2 | all-reduce | flops 1536 | bytes 12288 | tf_op jit(solution)/shard_map/pmax | solution.py:73
  44.6 0.2 fusion.3
  44.9 0.7 copy.30
  45.6 0.0 reduce-scatter.7.cloned.1.call-update
  45.7 0.0 copy-start.3
  45.7 0.0 reduce-scatter.5.cloned.1.call-start
  45.7 0.4 concatenate.19
  46.2 0.2 copy.21
  46.3 0.2 copy-done.3
  46.5 0.1 concatenate.20
  46.6 0.5 fusion.2
  47.0 0.0 copy-start.5
  47.1 0.0 copy-start.4
  47.1 1.1 copy.27
  48.2 0.0 reduce-scatter.5.cloned.1.call-update
  48.3 1.5 %collective-permute-start = (bf16[1,16,1536]{2,1,0:T(8,128)(2,1)S(1)}, bf16[1,16,1536]{2,1,0:T(8,128)(2,1)S(1)}, u32[]{:S(2)}, u32[]{:S(2)}) collective-permute-start(bf16[1,16,1536]{2,1,0:T(8,128)(2,1)S(1)} %copy-done.5), channel_id=1, source_target_pairs={{0,8},{8,16},{16,24},{24,0},{1,9},{9,17},{17,25},{25,1},{2,10},{10... | collective-permute-start | bytes 147464 | tf_op jit(solution)/shard_map/ppermute | solution.py:16
  49.8 24.8 %reduce-scatter.7.cloned.1.call-done = f32[16,12]{1,0:T(8,128)} async-done(((f32[128,12]{1,0:T(8,128)}), f32[16,12]{1,0:T(8,128)}) %reduce-scatter.7.cloned.1.call-update) | async-done | bytes 784 | tf_op jit(solution)/shard_map/reduce_scatter | solution.py:81
  74.6 0.0 collective-permute-done
  74.6 32.3 %reduce-scatter.5.cloned.1.call-done = f32[16,1536]{1,0:T(8,128)} async-done(((f32[128,1536]{1,0:T(8,128)}), f32[16,1536]{1,0:T(8,128)}) %reduce-scatter.5.cloned.1.call-update) | async-done | bytes 98320 | tf_op jit(solution)/shard_map/reduce_scatter | solution.py:80
  106.9 0.8 div.35
  107.7 1.6 %fusion.16 = (bf16[1,16,1536]{2,1,0:T(8,128)(2,1)}, bf16[16,1536]{1,0:T(8,128)(2,1)}) fusion(bf16[1,16,1536]{2,1,0:T(8,128)(2,1)S(1)} %collective-permute-done, f32[1536]{0:T(1024)S(1)} %reduce, f32[16,1536]{1,0:T(8,128)} %reduce-scatter.5.cloned.1.call-done, f32[2,8,12,128]{3,2,1,0:T(8,128)S(1)} %bitcast.30), kind=kLoop, calls=%fused_computation.20 | loop fusion | flops 172032 | bytes 350208 | tf_op jit(solution)/shard_map/convert_element_type | solution.py:87
  (10 shorter events, 0.1 us)
Async XLA Ops:
  7.2 67.4 %reduce-scatter.7.cloned.1.call-start = ((), (), s32[]{:S(2)}) async-start(), calls=%async_computation.3 | async-start | bytes 73728 | tf_op jit(solution)/shard_map/reduce_scatter | solution.py:81
  8.5 1.7 %copy-start.1 = (bf16[1,16,1536]{2,1,0:T(8,128)(2,1)S(1)}, bf16[1,16,1536]{2,1,0:T(8,128)(2,1)}, u32[]{:S(2)}) copy-start(bf16[1,16,1536]{2,1,0:T(8,128)(2,1)} %param.10) | copy-start | bytes 147460
  10.0 16.6 %copy-start.2 = (bf16[1,16,1536]{2,1,0:T(8,128)(2,1)S(1)}, bf16[1,16,1536]{2,1,0:T(8,128)(2,1)}, u32[]{:S(2)}) copy-start(bf16[1,16,1536]{2,1,0:T(8,128)(2,1)} %param.11) | copy-start | bytes 147460
  27.3 18.4 %copy-start = (bf16[1,192,1536]{2,1,0:T(8,128)(2,1)S(1)}, bf16[1,192,1536]{2,1,0:T(8,128)(2,1)}, u32[]{:S(2)}) copy-start(bf16[1,192,1536]{2,1,0:T(8,128)(2,1)} %param.14) | copy-start | bytes 1769476
  45.7 0.8 copy-start.3
  45.7 61.2 %reduce-scatter.5.cloned.1.call-start = ((), (), s32[]{:S(2)}) async-start(), calls=%async_computation.2 | async-start | bytes 884736 | tf_op jit(solution)/shard_map/reduce_scatter | solution.py:80
  47.0 1.2 %copy-start.5 = (bf16[1,16,1536]{2,1,0:T(8,128)(2,1)S(1)}, bf16[1,16,1536]{2,1,0:T(8,128)(2,1)}, u32[]{:S(2)}) copy-start(bf16[1,16,1536]{2,1,0:T(8,128)(2,1)} %param.9) | copy-start | bytes 147460
  47.1 2.7 %copy-start.4 = (f32[1,1536]{1,0:T(1,128)S(1)}, f32[1,1536]{1,0:T(1,128)}, u32[]{:S(2)}) copy-start(f32[1,1536]{1,0:T(1,128)} %param.15) | copy-start | bytes 18436
  48.3 26.3 %collective-permute-start = (bf16[1,16,1536]{2,1,0:T(8,128)(2,1)S(1)}, bf16[1,16,1536]{2,1,0:T(8,128)(2,1)S(1)}, u32[]{:S(2)}, u32[]{:S(2)}) collective-permute-start(bf16[1,16,1536]{2,1,0:T(8,128)(2,1)S(1)} %copy-done.5), channel_id=1, source_target_pairs={{0,8},{8,16},{16,24},{24,0},{1,9},{9,17},{17,25},{25,1},{2,10},{10... | collective-permute-start | bytes 147464 | tf_op jit(solution)/shard_map/ppermute | solution.py:16
Sparse Core Ops, SparseCore 0:
  45.8 28.7 reduce-scatter.6
  76.9 30.0 reduce-scatter.4
where the time goes:
time: 116 us
  waiting for transfers between devices  57.1 us (49%)
  blocking collectives  33.6 us (29%)
  between operations  15.5 us (13%)
  local copies, waits for them, and re-layouts  5.43 us (5%)
  other arithmetic  1.87 us (2%)
  starting transfers between devices  1.63 us (1%)
    reduce_scatter x1, waiting for transfers between devices, local(): lax.psum_scatter(partial_value, 'seq', scatter_dimension=0, tiled=True)  32.3 us
    reduce_scatter x1, waiting for transfers between devices, local(): lax.psum_scatter(weight_sums, 'seq', scatter_dimension=0, tiled=True)  24.8 us
    pmax x1, blocking collectives, local(): global_max = lax.pmax(local_max, 'seq')  17.3 us
    all_gather x1, blocking collectives, local(): everyone = lax.all_gather(queries, 'seq', axis=1, tiled=True)[0]  16.2 us
  transfers between devices with their start and end apart: 3, of which 2 were waited for; matrix products, arithmetic and copies ran while one was open for 2% of the time, Pallas kernels for 0%

commit v1 on v0

--- a/solution.py
+++ b/solution.py
@@ -8,6 +8,28 @@
 HDIM = 128
 TXT = 512
 FLOOR_SCORE = -1e30
+
+
+def in_order(tiles, dim):
+    tiles = jnp.moveaxis(tiles, 0, dim)
+    shape = tiles.shape
+    return tiles.reshape(*shape[:dim], shape[dim] * shape[dim + 1], *shape[dim + 2 :])
+
+
+def collect(x, axis, dim):
+    length = lax.axis_size(axis)
+    pairs = [(i, (i + 1) % length) for i in range(length)]
+    back = [(b, a) for a, b in pairs]
+    lower, upper = ([], [])
+    for hop in range(length - 1):
+        if hop % 2 == 0:
+            lower.append(lax.ppermute(lower[-1] if lower else x, axis, pairs))
+        else:
+            upper.append(lax.ppermute(upper[-1] if upper else x, axis, back))
+    blocks = jnp.stack([*lower[::-1], x, *upper])
+    shift = lax.axis_index(axis) - len(lower)
+    blocks = blocks[(jnp.arange(length) - shift) % length]
+    return in_order(blocks, dim)
 
 
 def passed_along(value, axis, steps):
@@ -56,7 +78,7 @@
     patch_length = row_count * lax.axis_size("seq")
     patch_index = patch_of_section[0]
     text_count = text_len[0]
-    everyone = lax.all_gather(queries, "seq", axis=1, tiled=True)[0]
+    everyone = collect(queries, "seq", 1)[0]
     stale_rows = stale_keys.shape[1]
     key_rows = jnp.concatenate([stale_keys[0], fresh_keys[0]], 0)
     value_rows = jnp.concatenate([stale_values[0], fresh_values[0]], 0)

time: 116 us -> 124 us (1.069)
  blocking collectives: 33.6 us -> 17.4 us
  starting transfers between devices: 1.63 us -> 14.2 us
  waiting for transfers between devices: 57.1 us -> 67.4 us
    all_gather x1 -> x0, blocking collectives: 16.2 us -> none  [local(): everyone = lax.all_gather(queries, 'seq', axis=1, tiled=True)[0]]
    ppermute x0 -> x7, starting transfers between devices: none -> 11.8 us  [the longest x3 11.3 us: collect(): upper.append(lax.ppermute(upper[-1] if upper else x, axis, back))]
    ppermute x0 -> x7, waiting for transfers between devices: none -> 9.44 us  [the longest x4 7.78 us: collect(): lower.append(lax.ppermute(lower[-1] if lower else x, axis, pairs))]
    ppermute x1, waiting for transfers between devices: 0.01 us -> 2.99 us  [passed_along(): return lax.ppermute(value, axis, pairs)]
    reduce_scatter x1, waiting for transfers between devices: 24.8 us -> 22.6 us  [local(): lax.psum_scatter(weight_sums, 'seq', scatter_dimension=0, tiled=True)]
  transfers between devices with their start and end apart: 3 -> 10, of which waited for: 2 -> 7; matrix products, arithmetic and copies ran while one was open for 2% -> 3% of each run, Pallas kernels for 0% -> 0%
where the time goes in v1:
time: 124 us
  waiting for transfers between devices  67.4 us (54%)
  blocking collectives  17.4 us (14%)
  between operations  15.6 us (13%)
  starting transfers between devices  14.2 us (11%)
  local copies, waits for them, and re-layouts  6.24 us (5%)
  other arithmetic  1.89 us (2%)
    reduce_scatter x1, waiting for transfers between devices, local(): lax.psum_scatter(partial_value, 'seq', scatter_dimension=0, tiled=True)  32.3 us
    reduce_scatter x1, waiting for transfers between devices, local(): lax.psum_scatter(weight_sums, 'seq', scatter_dimension=0, tiled=True)  22.6 us
    pmax x1, blocking collectives, local(): global_max = lax.pmax(local_max, 'seq')  17.4 us
    ppermute x3, starting transfers between devices, collect(): upper.append(lax.ppermute(upper[-1] if upper else x, axis, back))  11.3 us
    ppermute x4, waiting for transfers between devices, collect(): lower.append(lax.ppermute(lower[-1] if lower else x, axis, pairs))  7.78 us
    ppermute x1, waiting for transfers between devices, passed_along(): return lax.ppermute(value, axis, pairs)  2.99 us
  transfers between devices with their start and end apart: 10, of which 7 were waited for; matrix products, arithmetic and copies ran while one was open for 3% of the time, Pallas kernels for 0%

profile of v1, /device:TPU:0, one launch (start us, length us, event | category | flops | bytes accessed | tf_op | source)
XLA Modules:
  0.0 123.7 jit_solution(8661754062067174157)
XLA Ops:
  7.2 0.0 reduce-scatter.7.cloned.1.call-start
  7.2 0.5 collective-permute-start
  7.8 4.1 %collective-permute-start.4 = (bf16[1,16,1536]{2,1,0:T(8,128)(2,1)}, bf16[1,16,1536]{2,1,0:T(8,128)(2,1)S(1)}, u32[]{:S(2)}, u32[]{:S(2)}) collective-permute-start(bf16[1,16,1536]{2,1,0:T(8,128)(2,1)} %param.10), channel_id=1, source_target_pairs={{1,0},{2,1},{3,2},{4,3},{5,4},{6,5},{7,6},{0,7},{9,8},{10,9},{11,1... | collective-permute-start | bytes 147464 | tf_op jit(solution)/shard_map/ppermute | solution.py:28
  11.8 1.9 %collective-permute-done = bf16[1,16,1536]{2,1,0:T(8,128)(2,1)S(1)} collective-permute-done((bf16[1,16,1536]{2,1,0:T(8,128)(2,1)}, bf16[1,16,1536]{2,1,0:T(8,128)(2,1)S(1)}, u32[]{:S(2)}, u32[]{:S(2)}) %collective-permute-start) | collective-permute-done | bytes 49184 | tf_op jit(solution)/shard_map/ppermute | solution.py:26
  13.8 5.3 %collective-permute-done.1 = bf16[1,16,1536]{2,1,0:T(8,128)(2,1)S(1)} collective-permute-done((bf16[1,16,1536]{2,1,0:T(8,128)(2,1)S(1)}, bf16[1,16,1536]{2,1,0:T(8,128)(2,1)S(1)}, u32[]{:S(2)}, u32[]{:S(2)}) %collective-permute-start.1) | collective-permute-done | bytes 49184 | tf_op jit(solution)/shard_map/ppermute | solution.py:26
  20.4 3.6 %collective-permute-start.5 = (bf16[1,16,1536]{2,1,0:T(8,128)(2,1)S(1)}, bf16[1,16,1536]{2,1,0:T(8,128)(2,1)S(1)}, u32[]{:S(2)}, u32[]{:S(2)}) collective-permute-start(bf16[1,16,1536]{2,1,0:T(8,128)(2,1)S(1)} %collective-permute-done.4), channel_id=1, source_target_pairs={{1,0},{2,1},{3,2},{4,3},{5,4},{6,5},{7,6},{0,7},{9,8},{10,9},{11,1... | collective-permute-start | bytes 147464 | tf_op jit(solution)/shard_map/ppermute | solution.py:28
  24.0 0.6 collective-permute-done.2
  24.6 1.6 %concatenate.23 = bf16[192,12,128]{2,1,0:T(8,128)(2,1)S(1)} reshape(bf16[1,192,1536]{2,1,0:T(8,128)(2,1)} %param.13) | data formatting | bytes 1179648 | tf_op jit(solution)/shard_map/concatenate | solution.py:83
  26.2 0.2 copy.23
  26.3 0.1 concatenate.24
  26.4 0.4 concatenate.19
  26.9 0.2 copy.21
  27.0 0.2 copy-done.2
  27.2 0.1 concatenate.20
  27.3 3.6 %collective-permute-start.6 = (bf16[1,16,1536]{2,1,0:T(8,128)(2,1)S(1)}, bf16[1,16,1536]{2,1,0:T(8,128)(2,1)S(1)}, u32[]{:S(2)}, u32[]{:S(2)}) collective-permute-start(bf16[1,16,1536]{2,1,0:T(8,128)(2,1)S(1)} %collective-permute-done.5), channel_id=1, source_target_pairs={{1,0},{2,1},{3,2},{4,3},{5,4},{6,5},{7,6},{0,7},{9,8},{10,9},{11,1... | collective-permute-start | bytes 147464 | tf_op jit(solution)/shard_map/ppermute | solution.py:28
  31.0 1.7 %collective-permute-done.6 = bf16[1,16,1536]{2,1,0:T(8,128)(2,1)S(1)} collective-permute-done((bf16[1,16,1536]{2,1,0:T(8,128)(2,1)S(1)}, bf16[1,16,1536]{2,1,0:T(8,128)(2,1)S(1)}, u32[]{:S(2)}, u32[]{:S(2)}) %collective-permute-start.6) | collective-permute-done | bytes 49184 | tf_op jit(solution)/shard_map/ppermute | solution.py:28
  32.7 0.6 gather_fusion
  33.3 0.3 reshape_squeeze_reshape_transpose.3
  33.5 0.5 fusion.24
  34.1 17.4 %pmax.7 = f32[12,128]{1,0:T(8,128)S(1)} all-reduce(f32[12,128]{1,0:T(8,128)S(1)} %get-tuple-element.6), channel_id=1, replica_groups=mesh['section'=4,'seq'=8] {'seq'}, use_global_device_ids=true, to_apply=%region_1.2 | all-reduce | flops 1536 | bytes 12288 | tf_op jit(solution)/shard_map/pmax | solution.py:95
  51.5 0.2 fusion.2
  51.7 0.7 copy.28
  52.5 0.0 reduce-scatter.7.cloned.1.call-update
  52.5 0.0 reduce-scatter.5.cloned.1.call-start
  52.6 0.5 fusion.1
  53.1 1.2 copy.26
  54.3 2.3 %collective-permute-start.7 = (bf16[1,16,1536]{2,1,0:T(8,128)(2,1)S(1)}, bf16[1,16,1536]{2,1,0:T(8,128)(2,1)S(1)}, u32[]{:S(2)}, u32[]{:S(2)}) collective-permute-start(bf16[1,16,1536]{2,1,0:T(8,128)(2,1)S(1)} %copy-done.5), channel_id=1, source_target_pairs={{0,8},{8,16},{16,24},{24,0},{1,9},{9,17},{17,25},{25,1},{2,10},{10... | collective-permute-start | bytes 147464 | tf_op jit(solution)/shard_map/ppermute | solution.py:38
  56.6 3.0 %collective-permute-done.7 = bf16[1,16,1536]{2,1,0:T(8,128)(2,1)S(1)} collective-permute-done((bf16[1,16,1536]{2,1,0:T(8,128)(2,1)S(1)}, bf16[1,16,1536]{2,1,0:T(8,128)(2,1)S(1)}, u32[]{:S(2)}, u32[]{:S(2)}) %collective-permute-start.7) | collective-permute-done | bytes 49184 | tf_op jit(solution)/shard_map/ppermute | solution.py:38
  59.6 22.6 %reduce-scatter.7.cloned.1.call-done = f32[16,12]{1,0:T(8,128)} async-done(((f32[128,12]{1,0:T(8,128)}), f32[16,12]{1,0:T(8,128)}) %reduce-scatter.7.cloned.1.call-update) | async-done | bytes 784 | tf_op jit(solution)/shard_map/reduce_scatter | solution.py:103
  82.2 32.3 %reduce-scatter.5.cloned.1.call-done = f32[16,1536]{1,0:T(8,128)} async-done(((f32[128,1536]{1,0:T(8,128)}), f32[16,1536]{1,0:T(8,128)}) %reduce-scatter.5.cloned.1.call-update) | async-done | bytes 98320 | tf_op jit(solution)/shard_map/reduce_scatter | solution.py:102
  114.5 0.8 div.35
  115.3 1.6 %fusion.16 = (bf16[1,16,1536]{2,1,0:T(8,128)(2,1)}, bf16[16,1536]{1,0:T(8,128)(2,1)}) fusion(bf16[1,16,1536]{2,1,0:T(8,128)(2,1)S(1)} %collective-permute-done.7, f32[1536]{0:T(1024)S(1)} %reduce, f32[16,1536]{1,0:T(8,128)} %reduce-scatter.5.cloned.1.call-done, f32[2,8,12,128]{3,2,1,0:T(8,128)S(1)} %bitcast.45), kind=kLoop, calls=%fused_computation.21 | loop fusion | flops 172032 | bytes 350208 | tf_op jit(solution)/shard_map/convert_element_type | solution.py:109
  (34 shorter events, 0.2 us)
Async XLA Ops:
  7.2 75.0 %reduce-scatter.7.cloned.1.call-start = ((), (), s32[]{:S(2)}) async-start(), calls=%async_computation.3 | async-start | bytes 73728 | tf_op jit(solution)/shard_map/reduce_scatter | solution.py:103
  7.2 6.6 %collective-permute-start = (bf16[1,16,1536]{2,1,0:T(8,128)(2,1)}, bf16[1,16,1536]{2,1,0:T(8,128)(2,1)S(1)}, u32[]{:S(2)}, u32[]{:S(2)}) collective-permute-start(bf16[1,16,1536]{2,1,0:T(8,128)(2,1)} %param.10), channel_id=1, source_target_pairs={{0,1},{1,2},{2,3},{3,4},{4,5},{5,6},{6,7},{7,0},{8,9},{9,10},{10,1... | collective-permute-start | bytes 147464 | tf_op jit(solution)/shard_map/ppermute | solution.py:26
  7.8 12.6 %collective-permute-start.4 = (bf16[1,16,1536]{2,1,0:T(8,128)(2,1)}, bf16[1,16,1536]{2,1,0:T(8,128)(2,1)S(1)}, u32[]{:S(2)}, u32[]{:S(2)}) collective-permute-start(bf16[1,16,1536]{2,1,0:T(8,128)(2,1)} %param.10), channel_id=1, source_target_pairs={{1,0},{2,1},{3,2},{4,3},{5,4},{6,5},{7,6},{0,7},{9,8},{10,9},{11,1... | collective-permute-start | bytes 147464 | tf_op jit(solution)/shard_map/ppermute | solution.py:28
  13.8 5.3 %collective-permute-start.1 = (bf16[1,16,1536]{2,1,0:T(8,128)(2,1)S(1)}, bf16[1,16,1536]{2,1,0:T(8,128)(2,1)S(1)}, u32[]{:S(2)}, u32[]{:S(2)}) collective-permute-start(bf16[1,16,1536]{2,1,0:T(8,128)(2,1)S(1)} %collective-permute-done), channel_id=1, source_target_pairs={{0,1},{1,2},{2,3},{3,4},{4,5},{5,6},{6,7},{7,0},{8,9},{9,10},{10,1... | collective-permute-start | bytes 147464 | tf_op jit(solution)/shard_map/ppermute | solution.py:26
  19.1 5.5 %collective-permute-start.2 = (bf16[1,16,1536]{2,1,0:T(8,128)(2,1)S(1)}, bf16[1,16,1536]{2,1,0:T(8,128)(2,1)S(1)}, u32[]{:S(2)}, u32[]{:S(2)}) collective-permute-start(bf16[1,16,1536]{2,1,0:T(8,128)(2,1)S(1)} %collective-permute-done.1), channel_id=1, source_target_pairs={{0,1},{1,2},{2,3},{3,4},{4,5},{5,6},{6,7},{7,0},{8,9},{9,10},{10,1... | collective-permute-start | bytes 147464 | tf_op jit(solution)/shard_map/ppermute | solution.py:26
  20.4 6.9 %collective-permute-start.5 = (bf16[1,16,1536]{2,1,0:T(8,128)(2,1)S(1)}, bf16[1,16,1536]{2,1,0:T(8,128)(2,1)S(1)}, u32[]{:S(2)}, u32[]{:S(2)}) collective-permute-start(bf16[1,16,1536]{2,1,0:T(8,128)(2,1)S(1)} %collective-permute-done.4), channel_id=1, source_target_pairs={{1,0},{2,1},{3,2},{4,3},{5,4},{6,5},{7,6},{0,7},{9,8},{10,9},{11,1... | collective-permute-start | bytes 147464 | tf_op jit(solution)/shard_map/ppermute | solution.py:28
  24.6 6.4 %collective-permute-start.3 = (bf16[1,16,1536]{2,1,0:T(8,128)(2,1)S(1)}, bf16[1,16,1536]{2,1,0:T(8,128)(2,1)S(1)}, u32[]{:S(2)}, u32[]{:S(2)}) collective-permute-start(bf16[1,16,1536]{2,1,0:T(8,128)(2,1)S(1)} %collective-permute-done.2), channel_id=1, source_target_pairs={{0,1},{1,2},{2,3},{3,4},{4,5},{5,6},{6,7},{7,0},{8,9},{9,10},{10,1... | collective-permute-start | bytes 147464 | tf_op jit(solution)/shard_map/ppermute | solution.py:26
  24.6 1.8 %copy-start.1 = (bf16[1,16,1536]{2,1,0:T(8,128)(2,1)S(1)}, bf16[1,16,1536]{2,1,0:T(8,128)(2,1)}, u32[]{:S(2)}) copy-start(bf16[1,16,1536]{2,1,0:T(8,128)(2,1)} %param.11) | copy-start | bytes 147460
  24.6 1.8 %copy-start = (bf16[1,192,1536]{2,1,0:T(8,128)(2,1)S(1)}, bf16[1,192,1536]{2,1,0:T(8,128)(2,1)}, u32[]{:S(2)}) copy-start(bf16[1,192,1536]{2,1,0:T(8,128)(2,1)} %param.14) | copy-start | bytes 1769476
  26.4 0.8 copy-start.2
  26.9 4.1 %copy-start.3 = (bf16[1,16,1536]{2,1,0:T(8,128)(2,1)S(1)}, bf16[1,16,1536]{2,1,0:T(8,128)(2,1)}, u32[]{:S(2)}) copy-start(bf16[1,16,1536]{2,1,0:T(8,128)(2,1)} %param.10) | copy-start | bytes 147460
  27.3 5.3 %collective-permute-start.6 = (bf16[1,16,1536]{2,1,0:T(8,128)(2,1)S(1)}, bf16[1,16,1536]{2,1,0:T(8,128)(2,1)S(1)}, u32[]{:S(2)}, u32[]{:S(2)}) collective-permute-start(bf16[1,16,1536]{2,1,0:T(8,128)(2,1)S(1)} %collective-permute-done.5), channel_id=1, source_target_pairs={{1,0},{2,1},{3,2},{4,3},{5,4},{6,5},{7,6},{0,7},{9,8},{10,9},{11,1... | collective-permute-start | bytes 147464 | tf_op jit(solution)/shard_map/ppermute | solution.py:28
  52.5 62.0 %reduce-scatter.5.cloned.1.call-start = ((), (), s32[]{:S(2)}) async-start(), calls=%async_computation.2 | async-start | bytes 884736 | tf_op jit(solution)/shard_map/reduce_scatter | solution.py:102
  53.1 1.2 copy-start.5
  53.1 3.5 %copy-start.4 = (f32[1,1536]{1,0:T(1,128)S(1)}, f32[1,1536]{1,0:T(1,128)}, u32[]{:S(2)}) copy-start(f32[1,1536]{1,0:T(1,128)} %param.15) | copy-start | bytes 18436
  54.3 5.3 %collective-permute-start.7 = (bf16[1,16,1536]{2,1,0:T(8,128)(2,1)S(1)}, bf16[1,16,1536]{2,1,0:T(8,128)(2,1)S(1)}, u32[]{:S(2)}, u32[]{:S(2)}) collective-permute-start(bf16[1,16,1536]{2,1,0:T(8,128)(2,1)S(1)} %copy-done.5), channel_id=1, source_target_pairs={{0,8},{8,16},{16,24},{24,0},{1,9},{9,17},{17,25},{25,1},{2,10},{10... | collective-permute-start | bytes 147464 | tf_op jit(solution)/shard_map/ppermute | solution.py:38
Sparse Core Ops, SparseCore 0:
  52.6 29.4 reduce-scatter.6
  84.4 30.0 reduce-scatter.4
